TPU v7x, 128 devices: a whole 4x4x4 slice. The times are simulated.
128 devices in a mesh: doc: 8 (over z_lo, y), ctx: 16 (over x, z_hi, core).
Axes of the slice: x: 4, y: 4, z: 4 (z_hi: 2, z_lo: 2; z = z_hi * 2 + z_lo), core: 2. Of those that a mesh axis runs over, the one named last changes fastest.
Arguments:
- summary_cache: bfloat16 [8, 64, 512, 2048], P(None, 'doc', None, 'ctx'), may hold values from -4 to 4
- queries: bfloat16 [8, 4096, 4096], P('doc', 'ctx'), may hold values from -100 to 100
- section_counts: int32 [64], replicated, may hold values from 1 to 2
- summary_blocks: int32 [64, 2], replicated, may hold values from 1 to 2
Outputs:
- attended: bfloat16 [8, 4096, 4096], P('doc', 'ctx')
- relayed: bfloat16 [8, 8, 4096, 2048], P(None, 'doc', 'ctx')
All inputs are finite; a program needn't handle non-finite values.
Results may differ from a plain program's by a relative error of at most 0.0045.
Values may be sent and summed in bfloat16 or wider, within the bound.
A program may use at most 192 MiB of HBM per device.

v0:
```python
import functools
import math

import jax
import jax.numpy as jnp
from jax import lax
from jax.experimental import pallas as pl
from jax.experimental.pallas import tpu as pltpu
from jax.sharding import PartitionSpec as P

QH = 32
KVH = 8
HD = 128
BLOCK = 128
SECTIONS = 2
GROUP = 4
SUMLEN = 256


NEGATIVE = -1e30


MESH = pl.DeviceIdType.MESH


def kernel(
    rows,
    ctx,
    cache,
    queries,
    counts,
    blocks,
    attended,
    relayed,
    kv,
    mid,
    q_vmem,
    out_vmem,
    bias,
    s1,
    r1_first,
    r1,
    up_sem,
    down_sem,
    side_sem,
    kv_sem,
    s2,
    r2,
    local_sem,
):
    layers, _, slots, feat = cache.shape
    own = queries.shape[0]
    pieces = slots // own
    chips = ctx // 2
    me = lax.axis_index("doc")
    c = lax.axis_index("ctx")
    z = c // 2
    core = c % 2
    def seen(chip):
        return ((2 * chip + 2) * own + slots - 1) // slots

    barrier = pltpu.get_barrier_semaphore()
    for k in range(1, rows):
        pl.semaphore_signal(barrier, inc=1, device_id=((me + k) % rows, c), device_id_type=MESH)
    for k in range(1, ctx):
        pl.semaphore_signal(barrier, inc=1, device_id=(me, (c + k) % ctx), device_id_type=MESH)

    own_kv = pltpu.make_async_copy(
        cache.at[0, me], kv.at[c, pl.ds(pl.multiple_of(me * slots, slots), slots)], local_sem.at[0]
    )
    own_kv.start()
    q_copy = pltpu.make_async_copy(queries, q_vmem, local_sem.at[1])
    own_mid = pltpu.make_async_copy(cache.at[pl.ds(1, layers - 1), me], mid.at[:, me], local_sem.at[2])
    pl.semaphore_wait(barrier, rows - 1 + ctx - 1)

    def doc(ref, slice_index, j):
        return ref.at[slice_index, pl.ds(pl.multiple_of(j * slots, slots), slots)]

    def first_copy(j_to, j_from):
        return pltpu.make_async_remote_copy(
            src_ref=cache.at[0, j_to],
            dst_ref=doc(kv, c, j_from),
            send_sem=s1,
            recv_sem=r1_first.at[j_from],
            device_id=(j_to, c),
            device_id_type=MESH,
        )

    for k in range(1, rows):
        first_copy((me + k) % rows, me).start()
    own_mid.start()
    q_copy.start()

    def row_copy(l, j_to):
        return pltpu.make_async_remote_copy(
            src_ref=cache.at[l, j_to],
            dst_ref=mid.at[l - 1, me],
            send_sem=s1,
            recv_sem=r1.at[l],
            device_id=(j_to, c),
            device_id_type=MESH,
        )

    @pl.loop(1, layers)
    def _(l):
        for k in range(1, rows):
            row_copy(l, (me + k) % rows).start()

    def kv_copy(slice_index, j, sems, target):
        return pltpu.make_async_remote_copy(
            src_ref=doc(kv, slice_index, j),
            dst_ref=doc(kv, slice_index, j),
            send_sem=sems.at[slice_index, j],
            recv_sem=kv_sem.at[slice_index, j],
            device_id=(me, target),
            device_id_type=MESH,
        )

    def pass_on(slice_index, j, upward, downward):
        if upward:

            @pl.when(z < chips - 1)
            def _():
                kv_copy(slice_index, j, up_sem, c + 2).start()

        if downward:

            @pl.when((z > 0) & (j < seen(z - 1)))
            def _():
                kv_copy(slice_index, j, down_sem, c - 2).start()

        @pl.when(j < seen(z))
        def _():
            kv_copy(slice_index, j, side_sem, c + 1 - 2 * core).start()

    def spread(l, chosen):
        for k in chosen:
            t = (c + k) % ctx
            j = t // pieces
            h = t % pieces
            pltpu.make_async_remote_copy(
                src_ref=mid.at[l - 1, j, pl.ds(pl.multiple_of(h * own, own), own)],
                dst_ref=relayed.at[l, :, pl.ds(pl.multiple_of(c * feat, feat), feat)],
                send_sem=s2,
                recv_sem=r2,
                device_id=(me, t),
                device_id_type=MESH,
            ).start()

    def layer_step(l):
        arrived = mid.at[l - 1, pl.ds(0, rows - 1)]
        pltpu.make_async_copy(arrived, arrived, r1.at[l]).wait()
        spread(l, range(1, ctx))
        pltpu.make_async_copy(
            mid.at[l - 1, c // pieces, pl.ds(pl.multiple_of((c % pieces) * own, own), own)],
            relayed.at[l, :, pl.ds(pl.multiple_of(c * feat, feat), feat)],
            local_sem.at[3],
        ).start()

    own_kv.wait()
    pass_on(c, me, True, True)
    for k in range(1, rows):
        j = (me + k) % rows
        first_copy(me, j).wait_recv()
        pass_on(c, j, True, True)
    own_mid.wait()
    for step in range(1, chips):

        @pl.when(z >= step)
        def _():
            for k in range(rows):
                j = (me + k) % rows
                kv_copy(c - 2 * step, j, up_sem, c).wait_recv()
                pass_on(c - 2 * step, j, True, False)

        @pl.when(z + step < chips)
        def _():
            for k in range(rows):
                j = (me + k) % rows

                @pl.when(j < seen(z))
                def _():
                    kv_copy(c + 2 * step, j, down_sem, c).wait_recv()
                    pass_on(c + 2 * step, j, False, True)

        layer_step(step)

    @pl.loop(0, seen(z))
    def _(j):
        at = j * rows + me
        key = lax.broadcasted_iota(jnp.int32, (own, slots), 1)
        query = lax.broadcasted_iota(jnp.int32, (own, slots), 0)
        section = key // SUMLEN
        reach = jnp.zeros((own, slots), jnp.int32)
        for s in range(SECTIONS):
            reach = jnp.where((section == s) & (s < counts[at]), BLOCK * blocks[at, s], reach)
        allowed = (key - section * SUMLEN < reach) & (j * slots + key <= c * own + query)
        bias[j] = jnp.where(allowed, 0.0, NEGATIVE)

    for other in range(chips):
        slice_index = 2 * other + 1 - core

        @pl.loop(0, seen(z))
        def _(j):
            kv_copy(slice_index, j, side_sem, c).wait_recv()

    q_copy.wait()
    for t in range(ctx):
        pltpu.make_async_copy(
            kv.at[t, pl.ds(pl.multiple_of(c * own, own), own)],
            relayed.at[0, :, pl.ds(t * feat, feat)],
            local_sem.at[4],
        ).start()

    factor = math.log2(math.e) / math.sqrt(HD)

    @pl.loop(0, KVH)
    def _(k):
        @pl.when(k + chips < layers)
        def _():
            layer_step(k + chips)

        per = feat // HD
        key_slice = k // per
        value_slice = (KVH + k) // per
        lanes = pl.ds(pl.multiple_of((k % per) * HD, HD), HD)
        for i in range(GROUP):
            column = pl.ds(pl.multiple_of((k * GROUP + i) * HD, HD), HD)
            q = q_vmem[:, column]

            def block(j, state):
                top, total, acc = state
                at = pl.ds(pl.multiple_of(j * slots, slots), slots)
                s = lax.dot_general(
                    q, kv[key_slice, at, lanes], (((1,), (1,)), ((), ())), preferred_element_type=jnp.float32
                )
                s = s + bias[j]
                newest = jnp.maximum(top, jnp.max(s, axis=1, keepdims=True))
                w = jnp.exp2((s - newest) * factor)
                shrink = jnp.exp2((top - newest) * factor)
                total = total * shrink + jnp.sum(w, axis=1, keepdims=True)
                acc = acc * shrink + jnp.dot(
                    w.astype(jnp.bfloat16), kv[value_slice, at, lanes], preferred_element_type=jnp.float32
                )
                return newest, total, acc

            start = (
                jnp.full((own, 1), NEGATIVE, jnp.float32),
                jnp.zeros((own, 1), jnp.float32),
                jnp.zeros((own, HD), jnp.float32),
            )
            _, total, acc = lax.fori_loop(0, seen(z), block, start)
            out_vmem[:, column] = (acc / total).astype(jnp.bfloat16)

    out_copy = pltpu.make_async_copy(out_vmem, attended, local_sem.at[1])
    out_copy.start()

    @pl.loop(0, ctx)
    def _(t):
        @pl.loop(0, rows)
        def _(j):
            @pl.when(t % 2 == core)
            def _():
                chip = t // 2

                @pl.when((z < chips - 1) & (chip <= z))
                def _():
                    kv_copy(t, j, up_sem, c).wait_send()

                @pl.when((z > 0) & (j < seen(z - 1)) & (chip >= z))
                def _():
                    kv_copy(t, j, down_sem, c).wait_send()

                @pl.when(j < seen(z))
                def _():
                    kv_copy(t, j, side_sem, c).wait_send()

    def sized(ref, sem):
        return pltpu.make_async_copy(ref, ref, sem)

    sized(cache.at[:, pl.ds(0, rows - 1)], s1).wait()
    passed = relayed.at[pl.ds(1, layers - 1), :, pl.ds(0, (ctx - 1) * feat)]
    sized(passed, s2).wait()
    sized(passed, r2).wait()
    sized(relayed.at[pl.ds(1, layers - 1), :, pl.ds(0, feat)], local_sem.at[3]).wait()
    sized(relayed.at[0], local_sem.at[4]).wait()
    out_copy.wait()


def local(summary_cache, queries, section_counts, summary_blocks):
    rows = lax.axis_size("doc")
    ctx = lax.axis_size("ctx")
    layers, documents, slots, feat = summary_cache.shape
    own = queries.shape[1]
    dtype = summary_cache.dtype
    any_space = pl.BlockSpec(memory_space=pl.ANY)
    scalars = pl.BlockSpec(memory_space=pltpu.SMEM)
    dma = pltpu.SemaphoreType.DMA
    attended, relayed = pl.pallas_call(
        functools.partial(kernel, rows, ctx),
        out_shape=(
            jax.ShapeDtypeStruct(queries.shape[1:], dtype),
            jax.ShapeDtypeStruct((layers, own, ctx * feat), dtype),
        ),
        in_specs=[any_space, any_space, scalars, scalars],
        out_specs=(any_space, any_space),
        scratch_shapes=[
            pltpu.VMEM((ctx, rows * slots, feat), dtype),
            pltpu.VMEM((layers - 1, rows, slots, feat), dtype),
            pltpu.VMEM(queries.shape[1:], dtype),
            pltpu.VMEM(queries.shape[1:], dtype),
            pltpu.VMEM((rows, own, slots), jnp.float32),
            dma,
            dma((rows,)),
            dma((layers,)),
            dma((ctx, rows)),
            dma((ctx, rows)),
            dma((ctx, rows)),
            dma((ctx, rows)),
            dma,
            dma,
            dma((5,)),
        ],
        compiler_params=pltpu.CompilerParams(
            collective_id=0, has_side_effects=True, vmem_limit_bytes=60 * 1024 * 1024
        ),
    )(summary_cache, queries[0], section_counts, summary_blocks)
    return attended[None], relayed[:, None]


def solution(mesh):
    placed = (P(None, "doc", None, "ctx"), P("doc", "ctx", None), P(), P())
    return jax.shard_map(
        local,
        mesh=mesh,
        in_specs=placed,
        out_specs=(P("doc", "ctx", None), P(None, "doc", "ctx", None)),
        check_vma=False,
    )
```

profile of v0, /device:TPU:71, one launch (start us, length us, event | category | flops | bytes accessed | tf_op | source)
XLA Modules:
  0.0 518.9 jit_solution(14856478683067659997)
XLA Ops:
  0.6 1.4 copy.6.blocks
  2.0 505.4 %shard_map.59 = (bf16[256,4096]{1,0:T(8,128)(2,1)}, bf16[8,256,2048]{2,1,0:T(8,128)(2,1)}) custom-call(bf16[8,8,512,128]{3,2,1,0:T(8,128)(2,1)} %cache.1, bf16[256,4096]{1,0:T(8,128)(2,1)} %bitcast.7, s32[64]{0:T(128)} %counts.1, s32[64,2]{1,0:T(8,128)} %copy.6.blocks), custom_call_target="tpu_custom_call" | custom-call | tf_op jit(solution)/shard_map/pallas_call | solution.py:299
  507.4 3.1 copy.10
  510.5 8.4 %copy.11 = bf16[8,1,256,2048]{3,2,1,0:T(8,128)(2,1)} copy(bf16[8,1,256,2048]{3,2,1,0:T(8,128)(2,1)} %bitcast.5) | data formatting | bytes 16777216
where the time goes:
time: 519 us
  Pallas kernels  505 us (97%)
  local copies, waits for them, and re-layouts  13 us (3%)
    pallas_call x1, Pallas kernels, local(): pl.pallas_call(functools.partial(kernel, rows, ctx), out_shape=(jax.Shape...  505 us
    unnamed x3, local copies, waits for them, and re-layouts  13 us

commit v1 on v0

v1 whole, which is shorter than its diff:
```python
import functools
import math

import jax
import jax.numpy as jnp
from jax import lax
from jax.experimental import pallas as pl
from jax.experimental.pallas import tpu as pltpu
from jax.sharding import PartitionSpec as P

HD = 128
BLOCK = 128
SECTIONS = 2
GROUP = 4
SUMLEN = 256
XS = 4

NEGATIVE = -1e30
MESH = pl.DeviceIdType.MESH


def mult(v, n):
    return pl.multiple_of(v * n, n)


def kernel(
    rows,
    ctx,
    cache,
    queries,
    counts,
    blocks,
    attended,
    relayed,
    kv,
    mid,
    q_in,
    out_v,
    live,
    causal,
    kv_sem,
    q_sem,
    r1,
    r2,
    r0,
    ro,
    s_kv,
    s_fwd,
    s_q,
    s1,
    s2,
    s0,
    so,
):
    layers, _, slots, feat = cache.shape
    own = queries.shape[0]
    wide = GROUP * HD
    me = lax.axis_index("doc")
    c = lax.axis_index("ctx")
    x = c // 4
    zh = (c // 2) % 2
    core = c % 2

    def at(xx, z, o):
        return 4 * xx + 2 * z + o

    barrier = pltpu.get_barrier_semaphore()
    greeted = 0
    for k in range(rows):
        for dx in range(XS):
            for n in range(4):
                if (k, dx, n) == (0, 0, 0) or (k > 0 and dx % 2 == 1):
                    continue
                greeted += 1
                pl.semaphore_signal(
                    barrier,
                    inc=1,
                    device_id=((me + k) % rows, 4 * ((x + dx) % XS) + (c + n) % 4),
                    device_id_type=MESH,
                )

    kind = x // 2
    owner = at(x % 2 + 2 * core, zh, zh)
    head = 4 * (x % 2) + 2 * core + x // 2

    def remote(src, dst, send, recv, row, target):
        return pltpu.make_async_remote_copy(
            src_ref=src,
            dst_ref=dst,
            send_sem=send,
            recv_sem=recv,
            device_id=(row, target),
            device_id_type=MESH,
        )

    def sized(ref, sem):
        return pltpu.make_async_copy(ref, ref, sem)

    def doc(which, j):
        return kv.at[which, pl.ds(mult(j, slots), slots)]

    pl.semaphore_wait(barrier, greeted)

    @pl.when(owner != c)
    def _():
        remote(cache.at[0, me], doc(kind, me), s_kv, kv_sem.at[kind, me], me, owner).start()

    @pl.when(owner == c)
    def _():
        pltpu.make_async_copy(cache.at[0, me], doc(kind, me), kv_sem.at[kind, me]).start()

    for k in range(1, rows):
        g = (me + k) % rows
        remote(cache.at[0, g], doc(kind, me), s_kv, kv_sem.at[kind, me], g, owner).start()

    q_to = q_in.at[pl.ds(pl.multiple_of(512 * x + own * core, own), own)]
    for dx in (2, 1, 3, 0):
        for do in range(2):
            xx = (x + dx) % XS
            oo = (core + do) % 2
            k = 4 * (xx % 2) + 2 * oo + xx // 2
            src = queries.at[:, pl.ds(mult(k, wide), wide)]
            if dx == 0 and do == 0:
                pltpu.make_async_copy(src, q_to, q_sem.at[x]).start()
            else:
                remote(src, q_to, s_q, q_sem.at[x], me, at(xx, zh, oo)).start()

    def gather(l):
        dst = mid.at[l - 1, me // 2, :, pl.ds(mult(2 * zh + core, feat), feat)]
        for k in range(rows):
            g = (me + k) % rows
            for n in range(2):
                h = (core + n) % 2
                src = cache.at[l, g, pl.ds(mult(h, own), own)]
                copy = remote(src, dst, s1, r1.at[l], g, at(x, me % 2, h))
                if k == 0 and n == 0:

                    @pl.when(zh != me % 2)
                    def _():
                        copy.start()

                    @pl.when(zh == me % 2)
                    def _():
                        pltpu.make_async_copy(src, dst, r1.at[l]).start()
                else:
                    copy.start()

    def spread(l):
        sized(mid.at[l - 1], r1.at[l]).wait()
        dst = relayed.at[l, :, pl.ds(mult(x, wide), wide)]
        for dx in (2, 1, 3, 0):
            xx = (x + dx) % XS
            if dx:
                remote(mid.at[l - 1, xx], dst, s2, r2, me, at(xx, zh, core)).start()
            else:
                pltpu.make_async_copy(mid.at[l - 1, xx], dst, r2).start()

    @pl.loop(1, layers)
    def _(l):
        gather(l)

    key = lax.broadcasted_iota(jnp.int32, (8, slots), 1)

    @pl.loop(0, rows)
    def _(j):
        document = j * rows + me
        section = key // SUMLEN
        reach = jnp.zeros((8, slots), jnp.int32)
        for s in range(SECTIONS):
            reach = jnp.where(
                (section == s) & (s < counts[document]), BLOCK * blocks[document, s], reach
            )
        live[j] = jnp.where(key - section * SUMLEN < reach, 0.0, NEGATIVE)

    @pl.loop(0, slots // 8)
    def _(r):
        query = lax.broadcasted_iota(jnp.int32, (8, slots), 0) + 8 * r
        causal[pl.ds(mult(r, 8), 8)] = jnp.where(key <= query, 0.0, NEGATIVE)

    for k in range(rows):
        j = (me + k) % rows
        for which in range(2):
            block = doc(which, j)
            sized(block, kv_sem.at[which, j]).wait()

            @pl.when(zh == core)
            def _():
                remote(block, block, s_fwd, kv_sem.at[which, j], me, at(x, 1 - zh, core)).start()

    for which in range(2):
        for dx in (2, 1, 3, 0):
            for do in range(2):
                t = at((x + dx) % XS, zh, (core + do) % 2)
                src = kv.at[which, pl.ds(mult(t, own), own)]
                dst = relayed.at[0, :, pl.ds(pl.multiple_of(1024 * which + HD * head, HD), HD)]
                if dx == 0 and do == 0:
                    pltpu.make_async_copy(src, dst, r0).start()
                else:
                    remote(src, dst, s0, r0, me, t).start()

    factor = math.log2(math.e) / math.sqrt(HD)
    to = attended.at[:, pl.ds(mult(head, wide), wide)]

    for step, dx in enumerate((2, 1, 3, 0)):
        xt = (x + dx) % XS
        m = 2 * xt + zh
        row = pl.ds(mult(xt, slots), slots)
        sized(q_in.at[row], q_sem.at[xt]).wait()

        @pl.loop(0, GROUP)
        def _(i):
            l = 1 + 2 * step + i // 2

            @pl.when((i % 2 == 0) & (l < layers))
            def _():
                spread(l)

            column = pl.ds(mult(i, HD), HD)
            q = q_in[row, column]

            def block(j, state, bias):
                top, total, acc = state
                keys = pl.ds(mult(j, slots), slots)
                s = lax.dot_general(
                    q, kv[0, keys], (((1,), (1,)), ((), ())), preferred_element_type=jnp.float32
                )
                s = s + bias
                newest = jnp.maximum(top, jnp.max(s, axis=1, keepdims=True))
                w = jnp.exp2((s - newest) * factor)
                shrink = jnp.exp2((top - newest) * factor)
                total = total * shrink + jnp.sum(w, axis=1, keepdims=True)
                acc = acc * shrink + jnp.dot(
                    w.astype(jnp.bfloat16), kv[1, keys], preferred_element_type=jnp.float32
                )
                return newest, total, acc

            state = (
                jnp.full((slots, 1), NEGATIVE, jnp.float32),
                jnp.zeros((slots, 1), jnp.float32),
                jnp.zeros((slots, HD), jnp.float32),
            )
            state = lax.fori_loop(0, m, lambda j, st: block(j, st, live[j, 0:1]), state)
            _, total, acc = block(m, state, live[m, 0:1] + causal[...])
            out_v[row, column] = (acc / total).astype(jnp.bfloat16)

        for do in range(2):
            oo = (core + do) % 2
            src = out_v.at[pl.ds(pl.multiple_of(512 * xt + own * oo, own), own)]
            if dx == 0 and do == 0:
                pltpu.make_async_copy(src, to, ro).start()
            else:
                remote(src, to, so, ro, me, at(xt, zh, oo)).start()

    @pl.when(owner != c)
    def _():
        sized(cache.at[0, pl.ds(0, rows)], s_kv).wait()

    @pl.when(owner == c)
    def _():
        sized(cache.at[0, pl.ds(0, rows - 1)], s_kv).wait()

    @pl.when(zh == core)
    def _():
        sized(kv, s_fwd).wait()

    sized(q_in.at[pl.ds(0, 7 * own)], s_q).wait()

    @pl.when(zh != me % 2)
    def _():
        sized(cache.at[pl.ds(1, layers - 1)], s1).wait()

    @pl.when(zh == me % 2)
    def _():
        sized(cache.at[pl.ds(1, layers - 1), :, pl.ds(0, slots - slots // 16)], s1).wait()

    sized(mid.at[:, pl.ds(0, XS - 1)], s2).wait()
    sized(kv.at[:, pl.ds(0, 7 * own)], s0).wait()
    sized(out_v.at[pl.ds(0, 7 * own)], so).wait()
    sized(relayed.at[pl.ds(1, layers - 1)], r2).wait()
    sized(relayed.at[0], r0).wait()
    sized(attended, ro).wait()


def local(summary_cache, queries, section_counts, summary_blocks):
    rows = lax.axis_size("doc")
    ctx = lax.axis_size("ctx")
    layers, documents, slots, feat = summary_cache.shape
    own = queries.shape[1]
    wide = GROUP * HD
    dtype = summary_cache.dtype
    any_space = pl.BlockSpec(memory_space=pl.ANY)
    scalars = pl.BlockSpec(memory_space=pltpu.SMEM)
    dma = pltpu.SemaphoreType.DMA
    attended, relayed = pl.pallas_call(
        functools.partial(kernel, rows, ctx),
        out_shape=(
            jax.ShapeDtypeStruct(queries.shape[1:], dtype),
            jax.ShapeDtypeStruct((layers, own, ctx * feat), dtype),
        ),
        in_specs=[any_space, any_space, scalars, scalars],
        out_specs=(any_space, any_space),
        scratch_shapes=[
            pltpu.VMEM((2, rows * slots, feat), dtype),
            pltpu.VMEM((layers - 1, XS, own, wide), dtype),
            pltpu.VMEM((8 * own, wide), dtype),
            pltpu.VMEM((8 * own, wide), dtype),
            pltpu.VMEM((rows, 8, slots), jnp.float32),
            pltpu.VMEM((slots, slots), jnp.float32),
            dma((2, rows)),
            dma((XS,)),
            dma((layers,)),
            dma,
            dma,
            dma,
            dma,
            dma,
            dma,
            dma,
            dma,
            dma,
            dma,
        ],
        compiler_params=pltpu.CompilerParams(
            collective_id=0, has_side_effects=True, vmem_limit_bytes=60 * 1024 * 1024
        ),
    )(summary_cache, queries[0], section_counts, summary_blocks)
    return attended[None], relayed[:, None]


def solution(mesh):
    placed = (P(None, "doc", None, "ctx"), P("doc", "ctx", None), P(), P())
    return jax.shard_map(
        local,
        mesh=mesh,
        in_specs=placed,
        out_specs=(P("doc", "ctx", None), P(None, "doc", "ctx", None)),
        check_vma=False,
    )
```

time: 519 us -> 207 us (0.40)
  the two profiles are of different devices: /device:TPU:71 before, /device:TPU:112 now
where the time goes in v1:
time: 207 us; the launch traced here: 206 us
  Pallas kernels  193 us (93%)
  local copies, waits for them, and re-layouts  13 us (6%)
    pallas_call x1, Pallas kernels, local(): pl.pallas_call(functools.partial(kernel, rows, ctx), out_shape=(jax.Shape...  193 us
    unnamed x3, local copies, waits for them, and re-layouts  13 us

profile of v1, /device:TPU:112, one launch (start us, length us, event | category | flops | bytes accessed | tf_op | source)
XLA Modules:
  0.0 206.3 jit_solution(2773705975338582623)
XLA Ops:
  0.6 1.4 copy.6.blocks
  2.0 192.7 %shard_map.59 = (bf16[256,4096]{1,0:T(8,128)(2,1)}, bf16[8,256,2048]{2,1,0:T(8,128)(2,1)}) custom-call(bf16[8,8,512,128]{3,2,1,0:T(8,128)(2,1)} %cache.1, bf16[256,4096]{1,0:T(8,128)(2,1)} %bitcast.7, s32[64]{0:T(128)} %counts.1, s32[64,2]{1,0:T(8,128)} %copy.6.blocks), custom_call_target="tpu_custom_call" | custom-call | tf_op jit(solution)/shard_map/pallas_call | solution.py:294
  194.7 3.1 %copy.10 = bf16[1,256,4096]{2,1,0:T(8,128)(2,1)} copy(bf16[1,256,4096]{2,1,0:T(8,128)(2,1)} %bitcast.6) | data formatting | bytes 4194304
  197.8 8.4 %copy.11 = bf16[8,1,256,2048]{3,2,1,0:T(8,128)(2,1)} copy(bf16[8,1,256,2048]{3,2,1,0:T(8,128)(2,1)} %bitcast.5) | data formatting | bytes 16777216

commit v2 on v1

--- a/solution.py
+++ b/solution.py
@@ -127,10 +127,10 @@
 
     def gather(l):
         dst = mid.at[l - 1, me // 2, :, pl.ds(mult(2 * zh + core, feat), feat)]
-        for k in range(rows):
-            g = (me + k) % rows
-            for n in range(2):
-                h = (core + n) % 2
+        for n in range(2):
+            h = (core + n) % 2
+            for k in (1, 7, 2, 6, 3, 5, 4, 0):
+                g = (me + k) % rows
                 src = cache.at[l, g, pl.ds(mult(h, own), own)]
                 copy = remote(src, dst, s1, r1.at[l], g, at(x, me % 2, h))
                 if k == 0 and n == 0:
@@ -155,9 +155,7 @@
             else:
                 pltpu.make_async_copy(mid.at[l - 1, xx], dst, r2).start()
 
-    @pl.loop(1, layers)
-    def _(l):
-        gather(l)
+    gather(1)
 
     key = lax.broadcasted_iota(jnp.int32, (8, slots), 1)
 
@@ -177,15 +175,35 @@
         query = lax.broadcasted_iota(jnp.int32, (8, slots), 0) + 8 * r
         causal[pl.ds(mult(r, 8), 8)] = jnp.where(key <= query, 0.0, NEGATIVE)
 
-    for k in range(rows):
-        j = (me + k) % rows
-        for which in range(2):
-            block = doc(which, j)
-            sized(block, kv_sem.at[which, j]).wait()
-
-            @pl.when(zh == core)
-            def _():
-                remote(block, block, s_fwd, kv_sem.at[which, j], me, at(x, 1 - zh, core)).start()
+    def arrived(k, which):
+        block = doc(which, (me + k) % rows)
+        sized(block, kv_sem.at[which, (me + k) % rows]).wait()
+        return block
+
+    @pl.when(zh == core)
+    def _():
+        for k in (0, 7, 1, 6, 2, 5, 3, 4):
+            for which in range(2):
+                block = arrived(k, which)
+                remote(
+                    block, block, s_fwd, kv_sem.at[which, (me + k) % rows], me, at(x, 1 - zh, core)
+                ).start()
+
+    spread(1)
+
+    @pl.when(zh == core)
+    def _():
+        sized(kv, s_fwd).wait()
+
+    @pl.when(zh != core)
+    def _():
+        for k in range(rows):
+            for which in range(2):
+                arrived(k, which)
+
+    gather(2)
+    gather(3)
+    gather(4)
 
     for which in range(2):
         for dx in (2, 1, 3, 0):
@@ -209,11 +227,15 @@
 
         @pl.loop(0, GROUP)
         def _(i):
-            l = 1 + 2 * step + i // 2
-
-            @pl.when((i % 2 == 0) & (l < layers))
+            slot = GROUP * step + i
+
+            @pl.when(slot % 3 == 2)
             def _():
-                spread(l)
+                spread(2 + slot // 3)
+
+            @pl.when((slot % 3 == 2) & (slot < 9))
+            def _():
+                gather(5 + slot // 3)
 
             column = pl.ds(mult(i, HD), HD)
             q = q_in[row, column]
@@ -251,6 +273,8 @@
             else:
                 remote(src, to, so, ro, me, at(xt, zh, oo)).start()
 
+    spread(7)
+
     @pl.when(owner != c)
     def _():
         sized(cache.at[0, pl.ds(0, rows)], s_kv).wait()
@@ -258,10 +282,6 @@
     @pl.when(owner == c)
     def _():
         sized(cache.at[0, pl.ds(0, rows - 1)], s_kv).wait()
-
-    @pl.when(zh == core)
-    def _():
-        sized(kv, s_fwd).wait()
 
     sized(q_in.at[pl.ds(0, 7 * own)], s_q).wait()
 

time: 207 us -> 178 us (0.86)
  the two profiles are of different devices: /device:TPU:112 before, /device:TPU:71 now
where the time goes in v2:
time: 178 us; the launch traced here: 177 us
  Pallas kernels  163 us (92%)
  local copies, waits for them, and re-layouts  13 us (7%)
    pallas_call x1, Pallas kernels, local(): pl.pallas_call(functools.partial(kernel, rows, ctx), out_shape=(jax.Shape...  163 us
    unnamed x3, local copies, waits for them, and re-layouts  13 us

profile of v2, /device:TPU:71, one launch (start us, length us, event | category | flops | bytes accessed | tf_op | source)
XLA Modules:
  0.0 176.7 jit_solution(15754345574687889715)
XLA Ops:
  0.6 1.4 copy.6.blocks
  2.0 163.1 %shard_map.59 = (bf16[256,4096]{1,0:T(8,128)(2,1)}, bf16[8,256,2048]{2,1,0:T(8,128)(2,1)}) custom-call(bf16[8,8,512,128]{3,2,1,0:T(8,128)(2,1)} %cache.1, bf16[256,4096]{1,0:T(8,128)(2,1)} %bitcast.7, s32[64]{0:T(128)} %counts.1, s32[64,2]{1,0:T(8,128)} %copy.6.blocks), custom_call_target="tpu_custom_call" | custom-call | tf_op jit(solution)/shard_map/pallas_call | solution.py:314
  165.1 3.1 %copy.10 = bf16[1,256,4096]{2,1,0:T(8,128)(2,1)} copy(bf16[1,256,4096]{2,1,0:T(8,128)(2,1)} %bitcast.6) | data formatting | bytes 4194304
  168.3 8.4 %copy.11 = bf16[8,1,256,2048]{3,2,1,0:T(8,128)(2,1)} copy(bf16[8,1,256,2048]{3,2,1,0:T(8,128)(2,1)} %bitcast.5) | data formatting | bytes 16777216

commit v3 on v1

v3 whole, which is shorter than its diff:
```python
import functools
import math

import jax
import jax.numpy as jnp
from jax import lax
from jax.experimental import pallas as pl
from jax.experimental.pallas import tpu as pltpu
from jax.sharding import PartitionSpec as P

HD = 128
BLOCK = 128
SECTIONS = 2
GROUP = 4
SUMLEN = 256
XS = 4
YS = 4
ROUTES = ((1, 1), (3, 0), (2, 1), (0, 1), (1, 0), (3, 1), (2, 0), (0, 0))
SPREADS = ((2, 4), (3, 8), (4, 12), (5, 15), (6, 18))

NEGATIVE = -1e30
MESH = pl.DeviceIdType.MESH


def mult(v, n):
    return pl.multiple_of(v * n, n)


def kernel(
    rows,
    ctx,
    cache,
    queries,
    counts,
    blocks,
    attended,
    relayed,
    kv,
    mid,
    q_in,
    out_v,
    live,
    causal,
    kv_sem,
    q_sem,
    r1,
    r2,
    r0,
    ro,
    s_kv,
    s_q,
    s1,
    s2,
    s0,
    so,
):
    layers, _, slots, feat = cache.shape
    own = queries.shape[0]
    wide = GROUP * HD
    me = lax.axis_index("doc")
    c = lax.axis_index("ctx")
    x = c // 4
    zh = (c // 2) % 2
    core = c % 2

    def at(xx, z, o):
        return 4 * xx + 2 * z + o

    barrier = pltpu.get_barrier_semaphore()
    greeted = 0

    def greet(row, target):
        pl.semaphore_signal(barrier, inc=1, device_id=(row, target), device_id_type=MESH)

    for k in range(rows):
        row = (me + k) % rows
        for dx in (0, 2):
            for n in range(4):
                if (k, dx, n) != (0, 0, 0):
                    greet(row, 4 * ((x + dx) % XS) + (c + n) % 4)
                    greeted += 1
    for dx in (1, 3):
        for o in range(2):
            greet(me, at((x + dx) % XS, zh, o))
            greeted += 1

    def row_at(dy, dz):
        return YS * ((me // YS + dz) % 2) + (me + dy) % YS

    def head_of(xx, z, o):
        return 4 * (xx % 2) + 2 * o + (xx // 2 + z) % 2

    kind = x // 2
    near = x % 2 + 2 * core
    owners = (at(near, 0, zh), at((near + 2) % XS, 1, zh))
    head = head_of(x, zh, core)
    places = (
        (x, 1 - zh, 1 - zh, zh),
        ((x + 1) % XS, zh, 2, 3),
        ((x + 3) % XS, zh, 3, 2),
        (x, zh, zh, zh),
    )

    def remote(src, dst, send, recv, row, target):
        return pltpu.make_async_remote_copy(
            src_ref=src,
            dst_ref=dst,
            send_sem=send,
            recv_sem=recv,
            device_id=(row, target),
            device_id_type=MESH,
        )

    def sized(ref, sem):
        return pltpu.make_async_copy(ref, ref, sem)

    def doc(which, j):
        return kv.at[which, pl.ds(mult(j, slots), slots)]

    key = lax.broadcasted_iota(jnp.int32, (8, slots), 1)

    @pl.loop(0, rows)
    def _(j):
        document = j * rows + me
        section = key // SUMLEN
        reach = jnp.zeros((8, slots), jnp.int32)
        for s in range(SECTIONS):
            reach = jnp.where(
                (section == s) & (s < counts[document]), BLOCK * blocks[s, document], reach
            )
        live[j] = jnp.where(key - section * SUMLEN < reach, 0.0, NEGATIVE)

    @pl.loop(0, slots // 8)
    def _(r):
        query = lax.broadcasted_iota(jnp.int32, (8, slots), 0) + 8 * r
        causal[pl.ds(mult(r, 8), 8)] = jnp.where(key <= query, 0.0, NEGATIVE)

    pl.semaphore_wait(barrier, greeted)

    def first(owner, j):
        return remote(cache.at[0, j], doc(kind, me), s_kv, kv_sem.at[kind, me], j, owner)

    for owner in owners:

        @pl.when(owner != c)
        def _():
            first(owner, me).start()

        @pl.when(owner == c)
        def _():
            pltpu.make_async_copy(cache.at[0, me], doc(kind, me), kv_sem.at[kind, me]).start()

    for dy, dz in ROUTES[:-1]:
        for owner in owners:
            first(owner, row_at(dy, dz)).start()

    def ask():
        for n, (xx, z, _, slot) in enumerate(places):
            for do in range(2):
                oo = (core + do) % 2
                src = queries.at[:, pl.ds(mult(head_of(xx, z, oo), wide), wide)]
                dst = q_in.at[pl.ds(pl.multiple_of(slots * slot + own * core, own), own)]
                if n == len(places) - 1 and do == 0:
                    pltpu.make_async_copy(src, dst, q_sem.at[slot]).start()
                else:
                    remote(src, dst, s_q, q_sem.at[slot], me, at(xx, z, oo)).start()

    def gather(l):
        dst = mid.at[l - 1, me // 2, :, pl.ds(mult(2 * zh + core, feat), feat)]
        for n in range(2):
            h = (core + n) % 2
            for dy, dz in ROUTES:
                g = row_at(dy, dz)
                src = cache.at[l, g, pl.ds(mult(h, own), own)]
                copy = remote(src, dst, s1, r1.at[l], g, at(x, me % 2, h))
                if (dy, dz, n) == (0, 0, 0):

                    @pl.when(zh != me % 2)
                    def _():
                        copy.start()

                    @pl.when(zh == me % 2)
                    def _():
                        pltpu.make_async_copy(src, dst, r1.at[l]).start()
                else:
                    copy.start()

    def spread(l):
        sized(mid.at[l - 1], r1.at[l]).wait()
        dst = relayed.at[l, :, pl.ds(mult(x, wide), wide)]
        for dx in (2, 1, 3, 0):
            xx = (x + dx) % XS
            if dx:
                remote(mid.at[l - 1, xx], dst, s2, r2, me, at(xx, zh, core)).start()
            else:
                pltpu.make_async_copy(mid.at[l - 1, xx], dst, r2).start()

    ask()

    for which in range(2):
        for j in range(rows):
            sized(doc(which, j), kv_sem.at[which, j]).wait()

    for slot in range(XS):
        sized(q_in.at[pl.ds(slots * slot, slots)], q_sem.at[slot]).wait()

    @pl.loop(1, layers)
    def _(l):
        gather(l)

    for which in range(2):
        lanes = pl.ds(pl.multiple_of(1024 * which + HD * head, HD), HD)
        for n, (xx, z, _, _) in enumerate(places):
            for do in range(2):
                t = at(xx, z, (core + do) % 2)
                src = kv.at[which, pl.ds(mult(t, own), own)]
                dst = relayed.at[0, :, lanes]
                if n == len(places) - 1 and do == 0:
                    pltpu.make_async_copy(src, dst, r0).start()
                else:
                    remote(src, dst, s0, r0, me, t).start()

    spread(1)
    factor = math.log2(math.e) / math.sqrt(HD)
    to = attended.at[:, pl.ds(mult(head, wide), wide)]

    done = 0
    for n, (xt, zt, slot, _) in enumerate(places):
        m = 2 * xt + zt
        row = pl.ds(mult(slot, slots), slots)

        columns = [pl.ds(HD * i, HD) for i in range(GROUP)]

        def block(j, state, bias):
            keys = pl.ds(mult(j, slots), slots)
            shifted = []
            for column, (top, total, acc) in zip(columns, state):
                s = lax.dot_general(
                    q_in[row, column],
                    kv[0, keys],
                    (((1,), (1,)), ((), ())),
                    preferred_element_type=jnp.float32,
                )
                s = s + bias
                newest = jnp.maximum(top, jnp.max(s, axis=1, keepdims=True))
                w = jnp.exp2((s - newest) * factor)
                shrink = jnp.exp2((top - newest) * factor)
                total = total * shrink + jnp.sum(w, axis=1, keepdims=True)
                shifted.append((newest, total, acc * shrink, w.astype(jnp.bfloat16)))
            return tuple(
                (top, total, acc + jnp.dot(w, kv[1, keys], preferred_element_type=jnp.float32))
                for top, total, acc, w in shifted
            )

        def step_block(j, state):
            at_block = done + j
            for l, when in SPREADS:

                @pl.when(at_block == when)
                def _():
                    spread(l)

            return block(j, state, live[j, 0:1])

        state = (
            (
                jnp.full((slots, 1), NEGATIVE, jnp.float32),
                jnp.zeros((slots, 1), jnp.float32),
                jnp.zeros((slots, HD), jnp.float32),
            ),
        ) * GROUP
        state = lax.fori_loop(0, m, step_block, state)
        state = block(m, state, live[m, 0:1] + causal[...])
        for column, (_, total, acc) in zip(columns, state):
            out_v[row, column] = (acc / total).astype(jnp.bfloat16)
        done = done + m

        for do in range(2):
            oo = (core + do) % 2
            src = out_v.at[pl.ds(pl.multiple_of(slots * slot + own * oo, own), own)]
            if n == len(places) - 1 and do == 0:
                pltpu.make_async_copy(src, to, ro).start()
            else:
                remote(src, to, so, ro, me, at(xt, zt, oo)).start()

    for l, when in SPREADS:

        @pl.when(done <= when)
        def _():
            spread(l)

    for l in range(2 + len(SPREADS), layers):
        spread(l)

    @pl.when((kind == 0) & (zh == core))
    def _():
        sized(kv.at[:, pl.ds(0, (rows - 1) * slots + slots // 2)], s_kv).wait()

    @pl.when((kind == 1) | (zh != core))
    def _():
        sized(kv, s_kv).wait()

    sized(q_in.at[pl.ds(0, 7 * own)], s_q).wait()

    @pl.when(zh != me % 2)
    def _():
        sized(cache.at[pl.ds(1, layers - 1)], s1).wait()

    @pl.when(zh == me % 2)
    def _():
        sized(cache.at[pl.ds(1, layers - 1), :, pl.ds(0, slots - slots // 16)], s1).wait()

    sized(mid.at[:, pl.ds(0, XS - 1)], s2).wait()
    sized(kv.at[:, pl.ds(0, 7 * own)], s0).wait()
    sized(out_v.at[pl.ds(0, 7 * own)], so).wait()
    sized(relayed.at[pl.ds(1, layers - 1)], r2).wait()
    sized(relayed.at[0], r0).wait()
    sized(attended, ro).wait()


def place(attended, relayed, attended_out, relayed_out, sem):
    layers = relayed.shape[0]
    copies = [pltpu.make_async_copy(attended, attended_out, sem.at[layers])]
    copies += [pltpu.make_async_copy(relayed.at[l], relayed_out.at[l], sem.at[l]) for l in range(layers)]
    for copy in copies:
        copy.start()
    for copy in copies:
        copy.wait()


def local(summary_cache, queries, section_counts, summary_blocks):
    rows = lax.axis_size("doc")
    ctx = lax.axis_size("ctx")
    layers, documents, slots, feat = summary_cache.shape
    own = queries.shape[1]
    wide = GROUP * HD
    dtype = summary_cache.dtype
    any_space = pl.BlockSpec(memory_space=pl.ANY)
    hbm = pl.BlockSpec(memory_space=pltpu.MemorySpace.HBM)
    scalars = pl.BlockSpec(memory_space=pltpu.SMEM)
    dma = pltpu.SemaphoreType.DMA
    attended, relayed = pl.pallas_call(
        functools.partial(kernel, rows, ctx),
        out_shape=(
            pltpu.VMEM(queries.shape[1:], dtype),
            pltpu.VMEM((layers, own, ctx * feat), dtype),
        ),
        in_specs=[hbm, hbm, scalars, scalars],
        out_specs=(pl.BlockSpec(memory_space=pltpu.VMEM), pl.BlockSpec(memory_space=pltpu.VMEM)),
        scratch_shapes=[
            pltpu.VMEM((2, rows * slots, feat), dtype),
            pltpu.VMEM((layers - 1, XS, own, wide), dtype),
            pltpu.VMEM((8 * own, wide), dtype),
            pltpu.VMEM((8 * own, wide), dtype),
            pltpu.VMEM((rows, 8, slots), jnp.float32),
            pltpu.VMEM((slots, slots), jnp.float32),
            dma((2, rows)),
            dma((XS,)),
            dma((layers,)),
            dma,
            dma,
            dma,
            dma,
            dma,
            dma,
            dma,
            dma,
            dma,
        ],
        compiler_params=pltpu.CompilerParams(
            collective_id=0, has_side_effects=True, vmem_limit_bytes=52 * 1024 * 1024
        ),
    )(summary_cache, queries[0], section_counts, summary_blocks.T)
    vmem = pl.BlockSpec(memory_space=pltpu.VMEM)
    attended, relayed = pl.pallas_call(
        place,
        out_shape=(
            jax.ShapeDtypeStruct(attended.shape, dtype),
            jax.ShapeDtypeStruct(relayed.shape, dtype),
        ),
        in_specs=[vmem, vmem],
        out_specs=(any_space, any_space),
        scratch_shapes=[dma((layers + 1,))],
        compiler_params=pltpu.CompilerParams(vmem_limit_bytes=24 * 1024 * 1024),
    )(attended, relayed)
    return attended[None], relayed[:, None]


def solution(mesh):
    placed = (P(None, "doc", None, "ctx"), P("doc", "ctx", None), P(), P())
    return jax.shard_map(
        local,
        mesh=mesh,
        in_specs=placed,
        out_specs=(P("doc", "ctx", None), P(None, "doc", "ctx", None)),
        check_vma=False,
    )
```

time: 207 us -> 163 us (0.79)
  the two profiles are of different devices: /device:TPU:112 before, /device:TPU:5 now
where the time goes in v3:
time: 163 us
  Pallas kernels  162 us (99%)
    pallas_call x1, Pallas kernels, local(): pl.pallas_call(functools.partial(kernel, rows, ctx), out_shape=(pltpu.VME...  158 us
    pallas_call x1, Pallas kernels, local(): pl.pallas_call(place, out_shape=(jax.ShapeDtypeStruct(attended.shape, dty...  4.01 us

profile of v3, /device:TPU:5, one launch (start us, length us, event | category | flops | bytes accessed | tf_op | source)
XLA Modules:
  0.0 163.2 jit_solution(7737630017742837700)
XLA Ops:
  0.6 158.3 %shard_map.59 = (bf16[256,4096]{1,0:T(8,128)(2,1)S(1)}, bf16[8,256,2048]{2,1,0:T(8,128)(2,1)S(1)}) custom-call(bf16[8,8,512,128]{3,2,1,0:T(8,128)(2,1)} %cache.1, bf16[256,4096]{1,0:T(8,128)(2,1)} %bitcast.6, s32[64]{0:T(128)} %counts.1, s32[2,64]{1,0:T(2,128)} %bitcast.7), custom_call_target="tpu_custom_call" | custom-call | tf_op jit(solution)/shard_map/pallas_call | solution.py:342
  159.0 4.0 %shard_map.60 = (bf16[256,4096]{1,0:T(8,128)(2,1)}, bf16[8,256,2048]{2,1,0:T(8,128)(2,1)}) custom-call(bf16[256,4096]{1,0:T(8,128)(2,1)S(1)} %get-tuple-element.6.attended, bf16[8,256,2048]{2,1,0:T(8,128)(2,1)S(1)} %get-tuple-element.7.relayed), custom_call_target="tpu_custom_call" | custom-call | tf_op jit(solution)/shard_map/pallas_call | solution.py:375
